TPU v7x, 32 devices: a whole 2x2x4 slice. The times are simulated.
32 devices in a mesh: section: 4 (over y, x), dp: 8 (over z, core).
Axes of the slice: x: 2, y: 2, z: 4, core: 2. Of those that a mesh axis runs over, the one named last changes fastest.
Arguments:
- hidden_in: bfloat16 [2, 4, 4, 128, 4096], P(None, 'section', None, 'dp'), may hold values from -6 to 6
- out_grad: bfloat16 [4, 128, 4096], P(None, 'dp'), may hold values from -6 to 6
- gate_probs: float32 [2, 4, 4, 128, 2], P(None, 'section', None, 'dp'), may hold values from 0.1 to 1
- expert_ids: int32 [2, 4, 4, 128, 2], P(None, 'section', None, 'dp'), may hold values from 0 to 7, all different within a row
- task_ids: int32 [4, 8], P(None, 'dp'), may hold values from 0 to 1
- task_embed: float32 [2, 256], replicated, may hold values from -5 to 5
- slot_embed: float32 [2, 4, 8, 256], P(None, 'section'), may hold values from -5 to 5
- gen_down: bfloat16 [256, 65536], P(None, 'dp'), may hold values from -0.0078125 to 0.0078125
- gen_up: bfloat16 [256, 65536], P(None, 'dp'), may hold values from -0.09375 to 0.09375
Outputs:
- d_hidden: bfloat16 [4, 4, 128, 4096], P('section', None, 'dp')
- d_gen_down: float32 [256, 65536], P(None, 'dp')
- d_gen_up: float32 [256, 65536], P(None, 'dp')
- d_task_embed: float32 [2, 256], replicated
- d_slot_embed: float32 [2, 4, 8, 256], P(None, 'section')
Inputs may be any that keep to these rules, and one draw needn't show every extreme that they name: `expert_ids`: the two experts of a token differ.
All inputs are finite; a program needn't handle non-finite values.
Results may differ from a plain program's by a relative error of at most 0.025.
Values may be sent and summed in bfloat16 or wider, within the bound.
A program may use at most 128 MiB of HBM per device.

v0:
```python
import jax
import jax.numpy as jnp
from jax import lax
from jax.sharding import PartitionSpec as P

eps = 1e-05


def passed_along(shard, axis, by):
    count = lax.axis_size(axis)
    return lax.ppermute(shard, axis, [(i, (i + by) % count) for i in range(count)])


def column_weights(gates, choices_ids, task_hot, experts, rank):
    expert_hot = (choices_ids[:, :, None] == jnp.arange(experts, dtype=jnp.int32)).astype(
        jnp.float32
    )
    per_expert = jnp.sum(gates[:, :, None] * expert_hot, axis=1)
    table = task_hot[:, :, None] * per_expert[:, None, :]
    return jnp.repeat(table.reshape(table.shape[0], -1), rank, axis=1)


def layer_back(saved, cot_in, adapt_a, adapt_b, columns):
    values = saved.astype(jnp.float32)
    inv_rms = lax.rsqrt(jnp.mean(values * values, axis=-1, keepdims=True) + eps)
    normed_f = values * inv_rms
    normed = normed_f.astype(jnp.bfloat16)
    contract = (((1,), (1,)), ((), ()))
    low = lax.dot_general(normed, adapt_a, contract, preferred_element_type=jnp.float32)
    mixed_low = (columns * low).astype(jnp.bfloat16)
    back_low = lax.dot_general(cot_in, adapt_b, contract, preferred_element_type=jnp.float32)
    grad_low = (columns * back_low).astype(jnp.bfloat16)
    grad_norm = jnp.dot(grad_low, adapt_a, preferred_element_type=jnp.float32)
    grad_in = inv_rms * (
        grad_norm - normed_f * jnp.mean(grad_norm * normed_f, axis=-1, keepdims=True)
    )
    result = (cot_in.astype(jnp.float32) + grad_in).astype(jnp.bfloat16)
    return (result, normed, mixed_low, grad_low)


def keep_where(active, buffer, block_id, micro_id, fresh):
    return buffer.at[block_id, micro_id].set(jnp.where(active, fresh, buffer[block_id, micro_id]))


def on_device(
    hidden_in, out_grad, gate_probs, expert_ids, task_ids, task_embed, slot_embed, gen_down, gen_up
):
    high = lax.Precision.HIGHEST
    sections = lax.axis_size("section")
    section_id = lax.axis_index("section")
    blocks, _, micro_count, tok_rows, model_width = hidden_in.shape
    task_count, cond_width = task_embed.shape
    experts = slot_embed.shape[2]
    combos = task_count * experts
    pre_act = task_embed[None, :, None, :] + slot_embed[:, 0][:, None, :, :]
    conditions = jax.nn.silu(pre_act).reshape(blocks, combos, cond_width)
    gen_down_f = gen_down.astype(jnp.float32)
    gen_up_f = gen_up.astype(jnp.float32)
    shard_a = jnp.einsum("jcw,wf->jcf", conditions, gen_down_f, precision=high).astype(jnp.bfloat16)
    shard_b = jnp.einsum("jcw,wf->jcf", conditions, gen_up_f, precision=high).astype(jnp.bfloat16)
    full_a, full_b = (
        lax.all_gather(shard_a, "dp", axis=2, tiled=True),
        lax.all_gather(shard_b, "dp", axis=2, tiled=True),
    )
    adapt_a = full_a.reshape(blocks, -1, model_width)
    adapt_b = full_b.reshape(blocks, -1, model_width)
    ranks_all = adapt_a.shape[1]
    rank = ranks_all // combos
    total_items = blocks * micro_count

    def tick(tick_no, carry):
        incoming, normed_buf, cot_buf, low_buf, grad_low_buf, hidden_out = carry
        position = tick_no - (sections - 1 - section_id)
        active = (position >= 0) & (position < total_items)
        clipped = jnp.clip(position, 0, total_items - 1)
        block_id = blocks - 1 - clipped // micro_count
        micro_id = clipped % micro_count
        fresh_start = (section_id == sections - 1) & (clipped < micro_count)
        cot_in = jnp.where(fresh_start, out_grad[micro_id], incoming)
        task_hot = jnp.broadcast_to(
            (jnp.arange(task_count, dtype=jnp.int32) == task_ids[micro_id, 0]).astype(jnp.float32),
            (tok_rows, task_count),
        )
        columns = column_weights(
            gate_probs[block_id, 0, micro_id],
            expert_ids[block_id, 0, micro_id],
            task_hot,
            experts,
            rank,
        )
        result, normed, mixed_low, grad_low = layer_back(
            hidden_in[block_id, 0, micro_id], cot_in, adapt_a[block_id], adapt_b[block_id], columns
        )
        normed_buf = keep_where(active, normed_buf, block_id, micro_id, normed)
        cot_buf = keep_where(active, cot_buf, block_id, micro_id, cot_in)
        low_buf = keep_where(active, low_buf, block_id, micro_id, mixed_low)
        grad_low_buf = keep_where(active, grad_low_buf, block_id, micro_id, grad_low)
        hidden_out = hidden_out.at[micro_id].set(
            jnp.where(active & (block_id == 0), result, hidden_out[micro_id])
        )
        outgoing = passed_along(result, "section", -1)
        return (outgoing, normed_buf, cot_buf, low_buf, grad_low_buf, hidden_out)

    carry = (
        jnp.zeros((tok_rows, model_width), jnp.bfloat16),
        jnp.zeros((blocks, micro_count, tok_rows, model_width), jnp.bfloat16),
        jnp.zeros((blocks, micro_count, tok_rows, model_width), jnp.bfloat16),
        jnp.zeros((blocks, micro_count, tok_rows, ranks_all), jnp.bfloat16),
        jnp.zeros((blocks, micro_count, tok_rows, ranks_all), jnp.bfloat16),
        jnp.zeros((micro_count, tok_rows, model_width), jnp.bfloat16),
    )
    rows_contract = (((0,), (0,)), ((), ()))
    reduced = [None] * blocks
    start_tick = 0
    for block_id in reversed(range(blocks)):
        end_tick = (blocks - block_id) * micro_count + sections - 1
        carry = lax.fori_loop(start_tick, end_tick, tick, carry)
        start_tick = end_tick
        normed_all = carry[1][block_id].reshape(-1, model_width)
        cot_all = carry[2][block_id].reshape(-1, model_width)
        low_all = carry[3][block_id].reshape(-1, ranks_all)
        grad_low_all = carry[4][block_id].reshape(-1, ranks_all)
        grad_a = lax.dot_general(
            grad_low_all, normed_all, rows_contract, preferred_element_type=jnp.float32
        )
        grad_b = lax.dot_general(
            low_all, cot_all, rows_contract, preferred_element_type=jnp.float32
        )
        reduced[block_id] = lax.psum_scatter(
            (grad_a.reshape(combos, -1), grad_b.reshape(combos, -1)),
            "dp",
            scatter_dimension=1,
            tiled=True,
        )
    reduced_a = jnp.stack([pair[0] for pair in reduced])
    reduced_b = jnp.stack([pair[1] for pair in reduced])
    hidden_out = carry[5]
    grad_scale = 1.0 / (micro_count * tok_rows * lax.axis_size("dp"))
    reduced_a = reduced_a * grad_scale
    reduced_b = reduced_b * grad_scale
    part_down = jnp.einsum("jcw,jcf->wf", conditions, reduced_a, precision=high)
    part_up = jnp.einsum("jcw,jcf->wf", conditions, reduced_b, precision=high)
    d_gen_down, d_gen_up = lax.psum((part_down, part_up), "section")
    d_cond = jnp.einsum("jcf,wf->jcw", reduced_a, gen_down_f, precision=high)
    d_cond = d_cond + jnp.einsum("jcf,wf->jcw", reduced_b, gen_up_f, precision=high)
    sigmoid_pre = jax.nn.sigmoid(pre_act)
    d_pre = d_cond.reshape(pre_act.shape) * sigmoid_pre * (1.0 + pre_act * (1.0 - sigmoid_pre))
    d_pre_sum = lax.psum(d_pre, "dp")
    d_slot = jnp.sum(d_pre_sum, axis=1)
    d_task = lax.psum(jnp.sum(d_pre_sum, axis=(0, 2)), "section")
    return (hidden_out[None], d_gen_down, d_gen_up, d_task, d_slot[:, None])


def solution(mesh):
    placed = (
        P(None, "section", None, "dp", None),
        P(None, "dp", None),
        P(None, "section", None, "dp", None),
        P(None, "section", None, "dp", None),
        P(None, "dp"),
        P(),
        P(None, "section", None, None),
        P(None, "dp"),
        P(None, "dp"),
    )
    return jax.shard_map(
        on_device,
        mesh=mesh,
        in_specs=placed,
        out_specs=(
            P("section", None, "dp", None),
            P(None, "dp"),
            P(None, "dp"),
            P(),
            P(None, "section", None, None),
        ),
        check_vma=False,
    )
```

profile of v0, /device:TPU:0, one launch (start us, length us, event | category | flops | bytes accessed | tf_op | source)
XLA Modules:
  0.0 889.3 jit_solution(7068838330381721706)
XLA Ops:
  7.9 5.2 convolution_convert_fusion
  13.2 5.2 convolution_convert_fusion.1
  18.4 44.4 %all-gather.5.cloned.1.call-done = bf16[2,16,65536]{2,1,0:T(8,128)(2,1)} async-done(((bf16[2,16,8192]{2,1,0:T(8,128)(2,1)}), bf16[2,16,65536]{2,1,0:T(8,128)(2,1)}) %all-gather.5.cloned.1.call-update) | async-done | bytes 4194320 | tf_op jit(solution)/shard_map/all_gather | solution.py:62
  62.9 5.6 reshape.928
  68.5 42.3 %all-gather.3.cloned.1.call-done = bf16[2,16,65536]{2,1,0:T(8,128)(2,1)} async-done(((bf16[2,16,8192]{2,1,0:T(8,128)(2,1)}), bf16[2,16,65536]{2,1,0:T(8,128)(2,1)}) %all-gather.3.cloned.1.call-update) | async-done | bytes 4194320 | tf_op jit(solution)/shard_map/all_gather | solution.py:63
  110.8 5.6 reshape.927
  118.9 169.6 %while.60 = (s32[]{:T(128)}, bf16[16,4096]{1,0:T(8,128)(2,1)S(1)}, bf16[2,4,16,4096]{3,2,1,0:T(8,128)(2,1)S(1)}, bf16[2,4,16,4096]{3,2,1,0:T(8,128)(2,1)}, bf16[...) while((s32[]{:T(128)}, bf16[16,4096]{1,0:T(8,128)(2,1)S(1)}, ...), condition=%wide.region_6.7_spmd, body=%wide.region_0.6_spmd.sunk | while | flops 102532064 | bytes 10274211 | solution.py:117
  129.8 3.5 fusion.218
  133.3 2.1 fusion.219
  136.2 2.4 collective-permute-start
  140.7 3.5 fusion.222
  155.1 3.5 fusion.218
  158.6 2.1 fusion.219
  164.6 3.5 fusion.222
  178.9 3.5 fusion.218
  182.4 2.1 fusion.219
  188.5 3.5 fusion.222
  202.9 3.5 fusion.218
  206.4 2.1 fusion.219
  212.4 3.5 fusion.222
  226.8 3.5 fusion.218
  230.2 2.1 fusion.219
  237.2 3.5 fusion.222
  251.6 3.5 fusion.218
  255.1 2.1 fusion.219
  261.1 3.5 fusion.222
  275.5 3.5 fusion.218
  278.9 2.1 fusion.219
  285.0 3.5 fusion.222
  288.5 3.8 convolution_bitcast_fusion.2
  294.8 3.9 reshape.940
  298.8 99.0 %while.61 = (s32[]{:T(128)}, bf16[16,4096]{1,0:T(8,128)(2,1)S(1)}, bf16[2,4,16,4096]{3,2,1,0:T(8,128)(2,1)}, bf16[2,4,16,4096]{3,2,1,0:T(8,128)(2,1)}, bf16[2,4,...) while((s32[]{:T(128)}, bf16[16,4096]{1,0:T(8,128)(2,1)S(1)}, ...), condition=%wide.region_13.14_spmd, body=%wide.region_7.13_spmd.sunk | while | flops 102532064 | bytes 10276198 | solution.py:117
  309.6 3.4 fusion.231
  313.1 2.1 fusion.232
  317.6 2.3 fusion.234
  319.9 3.4 fusion.235
  334.1 3.5 fusion.231
  337.6 2.1 fusion.232
  343.2 2.2 fusion.234
  345.4 3.5 fusion.235
  359.7 3.4 fusion.231
  367.7 2.2 fusion.234
  370.0 3.4 fusion.235
  384.2 3.4 fusion.231
  392.1 2.2 fusion.234
  394.4 3.4 fusion.235
  397.8 4.0 convolution_bitcast_fusion.3
  401.8 4.0 reshape.937
  407.0 3.5 convolution_bitcast_fusion.5
  410.5 3.9 reshape.931
  414.5 3.5 convolution_bitcast_fusion.4
  418.0 4.0 reshape.934
  422.3 31.5 %reduce-scatter.9.cloned.1.call-done = f32[16,8192]{1,0:T(8,128)} async-done(((f32[16,65536]{1,0:T(8,128)}), f32[16,8192]{1,0:T(8,128)}) %reduce-scatter.9.cloned.1.call-update) | async-done | bytes 524304 | tf_op jit(solution)/shard_map/reduce_scatter | solution.py:129
  453.8 10.0 %convolution_bitcast_fusion = f32[256,8192]{1,0:T(8,128)} fusion(f32[1,16,8192]{2,1,0:T(8,128)} %bitcast.396, f32[1,16,8192]{2,1,0:T(8,128)} %bitcast.398, f32[2,8,256]{2,1,0:T(8,128)S(1)} %bitcast.406, f32[16,256]{1,0:T(8,128)S(1)} %copy-done.13), kind=kOutput, calls=%fused_computation.136 | convolution fusion | flops 805871616 | bytes 9469952 | tf_op jit(solution)/shard_map/jcw,jcf->wf/dot_general | solution.py:142
  463.8 40.5 %reduce-scatter.5.cloned.1.call-done = f32[16,8192]{1,0:T(8,128)} async-done(((f32[16,65536]{1,0:T(8,128)}), f32[16,8192]{1,0:T(8,128)}) %reduce-scatter.5.cloned.1.call-update) | async-done | bytes 524304 | tf_op jit(solution)/shard_map/reduce_scatter | solution.py:129
  504.3 50.6 %reduce-scatter.7.cloned.1.call-done = f32[16,8192]{1,0:T(8,128)} async-done(((f32[16,65536]{1,0:T(8,128)}), f32[16,8192]{1,0:T(8,128)}) %reduce-scatter.7.cloned.1.call-update) | async-done | bytes 524304 | tf_op jit(solution)/shard_map/reduce_scatter | solution.py:129
  554.9 10.0 %convolution_bitcast_fusion.1 = f32[256,8192]{1,0:T(8,128)} fusion(f32[1,16,8192]{2,1,0:T(8,128)} %bitcast.402, f32[1,16,8192]{2,1,0:T(8,128)} %bitcast.400, f32[2,8,256]{2,1,0:T(8,128)S(1)} %bitcast.407, f32[16,256]{1,0:T(8,128)S(1)} %copy-done.13), kind=kOutput, calls=%fused_computation.137 | convolution fusion | flops 805871616 | bytes 9469952 | tf_op jit(solution)/shard_map/jcw,jcf->wf/dot_general | solution.py:141
  566.1 6.0 fusion.118
  572.2 3.7 fusion.133
  575.9 26.0 %psum.30 = f32[2,2,8,256]{3,2,1,0:T(8,128)S(1)} all-reduce(f32[2,2,8,256]{3,2,1,0:T(8,128)S(1)} %fusion.133), channel_id=1, replica_groups=mesh['section'=4,'dp'=8] {'dp'}, use_global_device_ids=true, to_apply=%region_20.21 | all-reduce | flops 8192 | bytes 65536 | tf_op jit(solution)/shard_map/psum | solution.py:148
  602.5 11.0 %psum.31 = f32[2,256]{1,0:T(2,128)} all-reduce(f32[2,256]{1,0:T(2,128)S(1)} %get-tuple-element.972), channel_id=1, replica_groups=mesh['section'=4,'dp'=8] {'section'}, use_global_device_ids=true, to_apply=%region_22.23 | all-reduce | flops 512 | bytes 4096 | tf_op jit(solution)/shard_map/psum | solution.py:150
  613.5 257.7 %all-reduce.3.cloned.1.call-done = (f32[256,8192]{1,0:T(8,128)}, f32[256,8192]{1,0:T(8,128)}) async-done(((f32[256,8192]{1,0:T(8,128)}, f32[256,8192]{1,0:T(8,128)}), (f32[256,8192]{1,0:T(8,128)}, f32[256,8192]{1,0:T(8,128)})) %all-reduce.3.cloned.1.call-update) | async-done | bytes 16777232 | tf_op jit(solution)/shard_map/psum | solution.py:143
  871.2 7.8 copy.84
  879.0 3.4 copy.85
  (349 shorter events, 170.6 us)
Async XLA Ops:
  7.2 6.0 copy-start.10
  7.2 55.7 %all-gather.5.cloned.1.call-start = ((), (), s32[]{:S(2)}) async-start(), calls=%async_computation.5 | async-start | bytes 4718592 | tf_op jit(solution)/shard_map/all_gather | solution.py:62
  7.9 10.5 %copy-start.12 = (f32[16,256]{1,0:T(8,128)}, f32[16,256]{1,0:T(8,128)S(1)}, u32[]{:S(2)}) copy-start(f32[16,256]{1,0:T(8,128)S(1)} %broadcast_bitcast_fusion) | copy-start | bytes 49156
  13.1 97.6 %all-gather.3.cloned.1.call-start = ((), (), s32[]{:S(2)}) async-start(), calls=%async_computation.4 | async-start | bytes 4718592 | tf_op jit(solution)/shard_map/all_gather | solution.py:63
  18.4 403.9 %reduce-scatter.11.cloned.1.call-start = ((), (), s32[]{:S(2)}) async-start(), calls=%async_computation.9 | async-start | bytes 4718592 | tf_op jit(solution)/shard_map/reduce_scatter | solution.py:129
  68.5 50.4 %copy-start = (bf16[2,1,4,16,4096]{4,3,2,1,0:T(8,128)(2,1)S(1)}, bf16[2,1,4,16,4096]{4,3,2,1,0:T(8,128)(2,1)}, u32[]{:S(2)}) copy-start(bf16[2,1,4,16,4096]{4,3,2,1,0:T(8,128)(2,1)} %param.33) | copy-start | bytes 3145732
  68.5 50.4 %copy-start.4 = (bf16[4,16,4096]{2,1,0:T(8,128)(2,1)S(1)}, bf16[4,16,4096]{2,1,0:T(8,128)(2,1)}, u32[]{:S(2)}) copy-start(bf16[4,16,4096]{2,1,0:T(8,128)(2,1)} %param.34) | copy-start | bytes 1572868
  125.7 9.7 %copy-start.14 = (f32[16]{0:T(128)S(1)}, f32[16]{0:T(128)}, u32[]{:S(2)}) copy-start(f32[16]{0:T(128)} %add_rsqrt_fusion.4) | copy-start | bytes 196 | tf_op jit(solution)/shard_map/while
  136.2 8.0 collective-permute-start
  151.0 9.7 %copy-start.14 = (f32[16]{0:T(128)S(1)}, f32[16]{0:T(128)}, u32[]{:S(2)}) copy-start(f32[16]{0:T(128)} %add_rsqrt_fusion.4) | copy-start | bytes 196 | tf_op jit(solution)/shard_map/while
  161.5 6.6 collective-permute-start
  174.8 9.7 %copy-start.14 = (f32[16]{0:T(128)S(1)}, f32[16]{0:T(128)}, u32[]{:S(2)}) copy-start(f32[16]{0:T(128)} %add_rsqrt_fusion.4) | copy-start | bytes 196 | tf_op jit(solution)/shard_map/while
  185.3 6.7 collective-permute-start
  198.8 9.7 %copy-start.14 = (f32[16]{0:T(128)S(1)}, f32[16]{0:T(128)}, u32[]{:S(2)}) copy-start(f32[16]{0:T(128)} %add_rsqrt_fusion.4) | copy-start | bytes 196 | tf_op jit(solution)/shard_map/while
  209.3 6.6 collective-permute-start
  222.6 9.7 %copy-start.14 = (f32[16]{0:T(128)S(1)}, f32[16]{0:T(128)}, u32[]{:S(2)}) copy-start(f32[16]{0:T(128)} %add_rsqrt_fusion.4) | copy-start | bytes 196 | tf_op jit(solution)/shard_map/while
  233.1 7.6 collective-permute-start
  247.5 9.7 %copy-start.14 = (f32[16]{0:T(128)S(1)}, f32[16]{0:T(128)}, u32[]{:S(2)}) copy-start(f32[16]{0:T(128)} %add_rsqrt_fusion.4) | copy-start | bytes 196 | tf_op jit(solution)/shard_map/while
  258.0 6.6 collective-permute-start
  271.3 9.7 %copy-start.14 = (f32[16]{0:T(128)S(1)}, f32[16]{0:T(128)}, u32[]{:S(2)}) copy-start(f32[16]{0:T(128)} %add_rsqrt_fusion.4) | copy-start | bytes 196 | tf_op jit(solution)/shard_map/while
  281.8 6.7 collective-permute-start
  298.7 155.0 %reduce-scatter.9.cloned.1.call-start = ((), (), s32[]{:S(2)}) async-start(), calls=%async_computation.8 | async-start | bytes 4718592 | tf_op jit(solution)/shard_map/reduce_scatter | solution.py:129
  305.6 9.6 %copy-start.15 = (f32[16]{0:T(128)S(1)}, f32[16]{0:T(128)}, u32[]{:S(2)}) copy-start(f32[16]{0:T(128)} %add_rsqrt_fusion.5) | copy-start | bytes 196 | tf_op jit(solution)/shard_map/while
  315.9 7.4 collective-permute-start.1
  330.1 9.6 %copy-start.15 = (f32[16]{0:T(128)S(1)}, f32[16]{0:T(128)}, u32[]{:S(2)}) copy-start(f32[16]{0:T(128)} %add_rsqrt_fusion.5) | copy-start | bytes 196 | tf_op jit(solution)/shard_map/while
  340.5 8.4 collective-permute-start.1
  355.7 9.5 %copy-start.15 = (f32[16]{0:T(128)S(1)}, f32[16]{0:T(128)}, u32[]{:S(2)}) copy-start(f32[16]{0:T(128)} %add_rsqrt_fusion.5) | copy-start | bytes 196 | tf_op jit(solution)/shard_map/while
  365.9 7.5 collective-permute-start.1
  380.2 9.5 %copy-start.15 = (f32[16]{0:T(128)S(1)}, f32[16]{0:T(128)}, u32[]{:S(2)}) copy-start(f32[16]{0:T(128)} %add_rsqrt_fusion.5) | copy-start | bytes 196 | tf_op jit(solution)/shard_map/while
  390.5 7.3 collective-permute-start.1
  397.8 8.0 copy-start.3
  405.8 1.2 copy-start.5
  405.8 98.5 %reduce-scatter.5.cloned.1.call-start = ((), (), s32[]{:S(2)}) async-start(), calls=%async_computation.6 | async-start | bytes 4718592 | tf_op jit(solution)/shard_map/reduce_scatter | solution.py:129
  414.5 140.4 %reduce-scatter.7.cloned.1.call-start = ((), (), s32[]{:S(2)}) async-start(), calls=%async_computation.7 | async-start | bytes 4718592 | tf_op jit(solution)/shard_map/reduce_scatter | solution.py:129
  422.0 31.7 %copy-start.11 = (f32[2,1,8,256]{3,2,1,0:T(8,128)S(1)}, f32[2,1,8,256]{3,2,1,0:T(8,128)}, u32[]{:S(2)}) copy-start(f32[2,1,8,256]{3,2,1,0:T(8,128)} %param.39) | copy-start | bytes 49156
  422.0 31.7 %copy-start.13 = (f32[16,256]{1,0:T(8,128)S(1)}, f32[16,256]{1,0:T(8,128)}, u32[]{:S(2)}) copy-start(f32[16,256]{1,0:T(8,128)} %copy-done.12) | copy-start | bytes 49156
  422.0 449.2 %all-reduce.3.cloned.1.call-start = ((), (), s32[]{:S(2)}) async-start(), calls=%async_computation.10 | async-start | bytes 33554432 | tf_op jit(solution)/shard_map/psum | solution.py:143
  564.9 1.0 copy-start.8
  564.9 1.2 copy-start.9
  566.1 6.1 copy-start.1
  566.1 6.1 copy-start.6
  566.1 6.1 copy-start.7
  566.1 6.1 copy-start.16
  871.2 7.8 copy-start.2
Sparse Core Ops, SparseCore 0:
  13.2 49.5 all-gather.4
  65.1 45.6 all-gather.2
  298.8 47.9 reduce-scatter.10
  405.9 47.7 reduce-scatter.8
  455.9 48.3 reduce-scatter.4
  506.5 48.3 reduce-scatter.6
  565.1 306.0 all-reduce.2
where the time goes:
time: 894 us; the launch traced here: 889 us
  waiting for transfers between devices  467 us (52%)
  matrix products  154 us (17%)
  local copies, waits for them, and re-layouts  112 us (13%)
  other arithmetic  88.9 us (10%)
  blocking collectives  37 us (4%)
  starting transfers between devices  15.2 us (2%)
  between operations  14.3 us (2%)
    psum x1, waiting for transfers between devices, on_device(): d_gen_down, d_gen_up = lax.psum((part_down, part_up), 'section')  258 us
    reduce_scatter x4, waiting for transfers between devices, on_device(): lax.psum_scatter((grad_a.reshape(combos, -1), grad_b.reshape(combos, -1))...  123 us
    all_gather x1, waiting for transfers between devices, on_device(): lax.all_gather(shard_a, 'dp', axis=2, tiled=True)  44.4 us
    all_gather x1, waiting for transfers between devices, on_device(): lax.all_gather(shard_b, 'dp', axis=2, tiled=True)  42.3 us
    dot_general x11, matrix products, layer_back(): lax.dot_general(normed, adapt_a, contract, preferred_element_type=jnp.flo...  38 us
    dot_general x11, matrix products, layer_back(): lax.dot_general(cot_in, adapt_b, contract, preferred_element_type=jnp.flo...  38 us
    scatter x22, other arithmetic, keep_where(): buffer.at[block_id, micro_id]  33.1 us
    dynamic_slice x33, local copies, waits for them, and re-layouts, keep_where(): buffer[block_id, micro_id]  32.1 us
  transfers between devices with their start and end apart: 18, of which 6 were waited for; matrix products, arithmetic and copies ran while one was open for 21% of the time, Pallas kernels for 0%

commit v1 on v0

v1 whole, which is shorter than its diff:
```python
import functools

import jax
import jax.numpy as jnp
from jax import lax
from jax.experimental import pallas as pl
from jax.experimental.pallas import tpu as pltpu
from jax.sharding import PartitionSpec as P

eps = 1e-05
MESH = pl.DeviceIdType.MESH
nt = (((1,), (1,)), ((), ()))
tn = (((0,), (0,)), ((), ()))


def relay(
    sections, blocks, micro, chunk,
    hid, grad, cols, adapt,
    hid_out, xn_out, cot_out, low_out, glow_out,
    landed, made, wide, send_sem, recv_sem,
):
    me = lax.axis_index("section")
    below = lax.rem(me + sections - 1, sections)
    above = lax.rem(me + 1, sections)
    total = blocks * micro
    groups, _, rows, width = adapt.shape
    ranks = groups * rows
    spans = [pl.ds(at, chunk) for at in range(0, width, chunk)]

    barrier = pltpu.get_barrier_semaphore()
    for other in (below, above):
        pl.semaphore_signal(
            barrier, inc=1, device_id={"section": other}, device_id_type=MESH
        )
    pl.semaphore_wait(barrier, 2)

    def copy_of(item, slot):
        return pltpu.make_async_remote_copy(
            src_ref=made.at[item],
            dst_ref=landed.at[slot],
            send_sem=send_sem.at[item],
            recv_sem=recv_sem.at[slot],
            device_id={"section": below},
            device_id_type=MESH,
        )

    def step(item, carry):
        block = blocks - 1 - item // micro
        spot = block * micro + item % micro
        kind_a, kind_b = 2 * block, 2 * block + 1
        x = hid[spot].astype(jnp.float32)
        inv = lax.rsqrt(jnp.mean(x * x, axis=-1, keepdims=True) + eps)
        xn_out[spot] = (x * inv).astype(jnp.bfloat16)
        weights = cols[spot]
        low = jnp.zeros((x.shape[0], ranks), jnp.float32)
        for span in spans:
            low += lax.dot_general(
                xn_out[spot, :, span], adapt[:, kind_a, :, span].reshape(ranks, chunk), nt,
                preferred_element_type=jnp.float32,
            )
        low_out[spot] = (weights * low).astype(jnp.bfloat16)

        first = (me == sections - 1) & (item < micro)

        @pl.when(first)
        def _():
            landed[item] = grad[item % micro]

        @pl.when(jnp.logical_not(first))
        def _():
            copy_of(item, item).wait_recv()

        cot_out[spot] = landed[item]
        back = jnp.zeros((x.shape[0], ranks), jnp.float32)
        for span in spans:
            back += lax.dot_general(
                landed[item, :, span], adapt[:, kind_b, :, span].reshape(ranks, chunk), nt,
                preferred_element_type=jnp.float32,
            )
        glow = (weights * back).astype(jnp.bfloat16)
        glow_out[spot] = glow
        dots = jnp.zeros((x.shape[0], 1), jnp.float32)
        for span in spans:
            part = jnp.dot(
                glow, adapt[:, kind_a, :, span].reshape(ranks, chunk),
                preferred_element_type=jnp.float32,
            )
            wide[:, span] = part
            xf = hid[spot, :, span].astype(jnp.float32) * inv
            dots += jnp.sum(part * xf, axis=-1, keepdims=True)
        dots = dots * (1.0 / width)
        for span in spans:
            xf = hid[spot, :, span].astype(jnp.float32) * inv
            dx = landed[item, :, span].astype(jnp.float32) + inv * (wide[:, span] - xf * dots)
            made[item, :, span] = dx.astype(jnp.bfloat16)

        @pl.when(me > 0)
        def _():
            copy_of(item, item).start()

        @pl.when((me == 0) & (item < total - micro))
        def _():
            copy_of(item, item + micro).start()

        @pl.when(item >= total - micro)
        def _():
            hid_out[item % micro] = made[item]

        return carry

    lax.fori_loop(0, total, step, 0)

    def drain(item, carry):
        @pl.when((me > 0) | (item < total - micro))
        def _():
            copy_of(item, item).wait_send()

        return carry

    lax.fori_loop(0, total, drain, 0)


def on_device(
    hidden_in, out_grad, gate_probs, expert_ids, task_ids, task_embed, slot_embed, gen_down, gen_up
):
    sections, ways = lax.axis_size("section"), lax.axis_size("dp")
    section_id = lax.axis_index("section")
    blocks, _, micro, tok, width = hidden_in.shape
    tasks, cond_width = task_embed.shape
    experts = slot_embed.shape[2]
    combos = tasks * experts
    span = gen_down.shape[1]
    per = max(1, span // width)
    cuts = max(1, width // span)
    piece = span // per
    kinds = 2 * blocks
    total = blocks * micro

    slots = lax.all_gather(slot_embed[:, 0], "section", axis=0)
    pre_all = task_embed[None, None, :, None, :] + slots[:, :, None, :, :]
    sig_all = jax.nn.sigmoid(pre_all)
    cond_all = (pre_all * sig_all).reshape(-1, cond_width).astype(jnp.bfloat16)
    pre_own = task_embed[None, :, None, :] + slot_embed[:, 0][:, None, :, :]
    cond_own = jax.nn.silu(pre_own).reshape(-1, cond_width).astype(jnp.bfloat16)

    def made_from(gen):
        out = jnp.dot(cond_own, gen, preferred_element_type=jnp.float32).astype(jnp.bfloat16)
        out = out.reshape(blocks, combos, per, piece).transpose(0, 2, 1, 3)
        return out.reshape(blocks, per * combos, piece)

    shard = jnp.stack([made_from(gen_down), made_from(gen_up)], axis=1)
    shard = shard.reshape(1, kinds, per * combos, piece)
    adapt = lax.all_gather(shard, "dp", axis=0, tiled=True)
    if cuts > 1:
        adapt = adapt.reshape(ways // cuts, cuts, kinds, combos, piece).transpose(0, 2, 3, 1, 4)
        adapt = adapt.reshape(ways // cuts, kinds, combos, width)
    groups = adapt.shape[0]
    ranks = groups * per * combos

    hot = (expert_ids[:, 0][..., None] == jnp.arange(experts, dtype=jnp.int32)).astype(jnp.float32)
    per_expert = jnp.sum(gate_probs[:, 0][..., None] * hot, axis=3)
    task_hot = (task_ids == jnp.arange(tasks, dtype=jnp.int32)).astype(jnp.float32)
    table = task_hot[None, :, None, :, None] * per_expert[:, :, :, None, :]
    cols = jnp.tile(table.reshape(total, tok, combos), (1, 1, ranks // combos))

    whole = pl.BlockSpec(memory_space=pltpu.VMEM)
    bf = jnp.bfloat16
    hid_out, xn, cot, low, glow = pl.pallas_call(
        functools.partial(relay, sections, blocks, micro, min(width, 1024)),
        out_shape=(
            jax.ShapeDtypeStruct((micro, tok, width), bf),
            jax.ShapeDtypeStruct((total, tok, width), bf),
            jax.ShapeDtypeStruct((total, tok, width), bf),
            jax.ShapeDtypeStruct((total, tok, ranks), bf),
            jax.ShapeDtypeStruct((total, tok, ranks), bf),
        ),
        in_specs=[whole] * 4,
        out_specs=(whole,) * 5,
        scratch_shapes=[
            pltpu.VMEM((total, tok, width), bf),
            pltpu.VMEM((total, tok, width), bf),
            pltpu.VMEM((tok, width), jnp.float32),
            pltpu.SemaphoreType.DMA((total,)),
            pltpu.SemaphoreType.DMA((total,)),
        ],
        compiler_params=pltpu.CompilerParams(
            collective_id=1, has_side_effects=True, vmem_limit_bytes=40 << 20
        ),
        name="relay",
    )(hidden_in.reshape(total, tok, width), out_grad, cols, adapt)

    scale = 1.0 / (micro * tok * ways)

    def grads(left, right):
        out = lax.dot_general(
            left.reshape(-1, ranks), right.reshape(-1, width), tn,
            preferred_element_type=jnp.float32,
        )
        out = (out * scale).astype(bf)
        if cuts > 1:
            out = out.reshape(ways // cuts, combos, cuts, piece).transpose(0, 2, 1, 3)
        return out.reshape(ways, 1, per * combos, piece)

    reduced = []
    for block in range(blocks):
        at = slice(block * micro, (block + 1) * micro)
        pair = jnp.concatenate([grads(glow[at], xn[at]), grads(low[at], cot[at])], axis=1)
        reduced.append(lax.psum_scatter(pair, "dp", scatter_dimension=0, tiled=True))
    own = jnp.concatenate(reduced, axis=0)
    every = lax.all_gather(own, "section", axis=0, tiled=True)
    every = every.reshape(sections * blocks, 2, per, combos, piece)
    every = every.transpose(1, 0, 3, 2, 4).reshape(2, -1, span)
    part = jnp.zeros((), jnp.float32)
    d_gens = []
    for which, gen in ((0, gen_down), (1, gen_up)):
        d_gens.append(
            lax.dot_general(cond_all, every[which], tn, preferred_element_type=jnp.float32)
        )
        part = part + lax.dot_general(every[which], gen, nt, preferred_element_type=jnp.float32)
    d_pre = part.reshape(pre_all.shape) * sig_all * (1.0 + pre_all * (1.0 - sig_all))
    sums = jnp.concatenate(
        [
            jnp.sum(d_pre, axis=2).reshape(-1, cond_width),
            jnp.sum(d_pre, axis=(0, 1, 3)),
        ]
    )
    sums = lax.psum(sums, "dp")
    d_task = sums[-tasks:]
    d_slot = lax.dynamic_slice_in_dim(
        sums, section_id * blocks * experts, blocks * experts
    ).reshape(blocks, 1, experts, cond_width)
    return (hid_out[None], d_gens[0], d_gens[1], d_task, d_slot)


def solution(mesh):
    placed = (
        P(None, "section", None, "dp", None),
        P(None, "dp", None),
        P(None, "section", None, "dp", None),
        P(None, "section", None, "dp", None),
        P(None, "dp"),
        P(),
        P(None, "section", None, None),
        P(None, "dp"),
        P(None, "dp"),
    )
    return jax.shard_map(
        on_device,
        mesh=mesh,
        in_specs=placed,
        out_specs=(
            P("section", None, "dp", None),
            P(None, "dp"),
            P(None, "dp"),
            P(),
            P(None, "section", None, None),
        ),
        check_vma=False,
    )
```

time: 894 us -> 395 us (0.44)
  waiting for transfers between devices: 467 us -> 261 us
  matrix products: 154 us -> 21.3 us
  local copies, waits for them, and re-layouts: 112 us -> 22 us
  other arithmetic: 88.9 us -> 8.76 us
  Pallas kernels: 0 us -> 57.9 us
  blocking collectives: 37 us -> 8.39 us
  starting transfers between devices: 15.2 us -> 0.21 us
    psum x1, waiting for transfers between devices: 258 us -> 40.9 us  [on_device(): sums = lax.psum(sums, 'dp')]
    dot_general x43 -> x10, matrix products: 154 us -> 21.3 us  [the longest x2 9.34 us: on_device(): lax.dot_general(cond_all, every[which], tn, preferred_element_type=jnp.fl...]
    pallas_call x0 -> x1, Pallas kernels: none -> 57.9 us  [on_device(): pl.pallas_call(functools.partial(relay, sections, blocks, micro, min(widt...]
    dynamic_slice x55 -> x0, local copies, waits for them, and re-layouts: 45.9 us -> none  [the longest x33 32.1 us: keep_where(): buffer[block_id, micro_id]]
    scatter x33 -> x0, other arithmetic: 41.6 us -> none  [the longest x22 33.1 us: keep_where(): buffer.at[block_id, micro_id]]
    all_gather x2, waiting for transfers between devices: 86.7 us -> 127 us  [the longest x1 83.9 us: on_device(): adapt = lax.all_gather(shard, 'dp', axis=0, tiled=True)]
    psum x2 -> x0, blocking collectives: 37 us -> none  [the longest x1 26 us: on_device(): d_pre_sum = lax.psum(d_pre, 'dp')]
    another operation x22 -> x1, other arithmetic: 30.4 us -> 0.1 us  [on_device(): shard = jnp.stack([made_from(gen_down), made_from(gen_up)], axis=1)]
  transfers between devices with their start and end apart: 18 -> 5, of which waited for: 6 -> 5; matrix products, arithmetic and copies ran while one was open for 21% -> 4% of each run, Pallas kernels for 0% -> 0%
where the time goes in v1:
time: 395 us; the launch traced here: 393 us
  waiting for transfers between devices  261 us (66%)
  Pallas kernels  57.9 us (15%)
  local copies, waits for them, and re-layouts  22 us (6%)
  matrix products  21.3 us (5%)
  between operations  14.1 us (4%)
  other arithmetic  8.76 us (2%)
  blocking collectives  8.39 us (2%)
    reduce_scatter x2, waiting for transfers between devices, on_device(): lax.psum_scatter(pair, 'dp', scatter_dimension=0, tiled=True)  92.9 us
    all_gather x1, waiting for transfers between devices, on_device(): adapt = lax.all_gather(shard, 'dp', axis=0, tiled=True)  83.9 us
    pallas_call x1, Pallas kernels, on_device(): pl.pallas_call(functools.partial(relay, sections, blocks, micro, min(widt...  57.9 us
    all_gather x1, waiting for transfers between devices, on_device(): every = lax.all_gather(own, 'section', axis=0, tiled=True)  42.8 us
    psum x1, waiting for transfers between devices, on_device(): sums = lax.psum(sums, 'dp')  40.9 us
    unnamed x31, local copies, waits for them, and re-layouts  9.37 us
    dot_general x2, matrix products, on_device(): lax.dot_general(cond_all, every[which], tn, preferred_element_type=jnp.fl...  9.34 us
    all_gather x1, blocking collectives, on_device(): slots = lax.all_gather(slot_embed[:, 0], 'section', axis=0)  8.39 us
  transfers between devices with their start and end apart: 5, of which 5 were waited for; matrix products, arithmetic and copies ran while one was open for 4% of the time, Pallas kernels for 0%

profile of v1, /device:TPU:0, one launch (start us, length us, event | category | flops | bytes accessed | tf_op | source)
XLA Modules:
  0.0 393.2 jit_solution(4558540322249004153)
XLA Ops:
  7.2 0.0 all-gather.4.cloned.1.call-start
  7.2 0.7 broadcast_add_fusion
  8.0 3.0 convolution_convert_fusion
  11.0 0.4 reshape.122
  11.4 0.3 copy.68
  11.7 3.0 convolution_convert_fusion.1
  14.7 0.0 copy-start.13
  14.7 0.0 copy-start.11
  14.7 0.0 copy-start.12
  14.7 0.4 reshape.121
  15.1 0.3 copy.67
  15.4 0.0 copy-start.1
  15.4 0.1 pad_maximum_fusion.2
  15.5 1.0 copy.69
  16.6 0.0 all-gather.4.cloned.1.call-update
  16.6 0.0 reduce-scatter.5.cloned.1.call-start
  16.7 0.1 fusion.22
  16.7 0.1 mul.78
  16.8 0.1 mul.79
  16.9 0.1 broadcast_multiply_fusion
  17.0 0.1 copy.66
  17.1 0.1 tile.8
  17.2 0.4 tile.9.cols
  17.6 83.9 %all-gather.4.cloned.1.call-done.adapt = bf16[8,4,32,4096]{3,2,1,0:T(8,128)(2,1)} async-done(((bf16[1,4,32,4096]{3,2,1,0:T(8,128)(2,1)}), bf16[8,4,32,4096]{3,2,1,0:T(8,128)(2,1)}) %all-gather.4.cloned.1.call-update) | async-done | bytes 8388624 | tf_op jit(solution)/shard_map/all_gather | solution.py:153
  101.5 3.4 copy-done
  104.9 57.9 %relay.1 = (bf16[4,16,4096]{2,1,0:T(8,128)(2,1)S(1)}, bf16[8,16,4096]{2,1,0:T(8,128)(2,1)S(1)}, bf16[8,16,4096]{2,1,0:T(8,128)(2,1)S(1)}, bf16[8,16,256]{2,1,0:T(8,128)(2,1)S(1)}, bf16[8,16,256]{2,1,0:T(8,128)(2,1)S(1)}) custom-call(bf16[8,16,4096]{2,1,0:T(8,128)(2,1)S(1)} %bitcast.96, bf16[4,16,4096]{2,1,0:T(8,128)(2,1)S(1)} %copy-done.2, ...), custom_call_target="tpu_custom_call" | custom-call | tf_op jit(solution)/shard_map/relay/pallas_call | solution.py:168
  162.8 0.7 fusion.6
  163.5 0.7 fusion.7
  164.3 2.4 pad_maximum_fusion.1
  166.7 0.0 reduce-scatter.5.cloned.1.call-update
  166.7 0.0 reduce-scatter.3.cloned.1.call-start
  166.7 1.1 copy-done.4
  167.9 0.7 fusion.4
  168.6 0.7 fusion.5
  169.3 2.4 pad_maximum_fusion
  171.7 0.0 reduce-scatter.3.cloned.1.call-update
  171.7 0.0 all-gather.6.cloned.1.call-start
  171.8 41.6 %reduce-scatter.5.cloned.1.call-done = bf16[1,2,32,4096]{3,2,1,0:T(8,128)(2,1)} async-done(((bf16[8,2,32,4096]{3,2,1,0:T(8,128)(2,1)}), bf16[1,2,32,4096]{3,2,1,0:T(8,128)(2,1)}) %reduce-scatter.5.cloned.1.call-update) | async-done | bytes 524304 | tf_op jit(solution)/shard_map/reduce_scatter | solution.py:208
  213.4 51.3 %reduce-scatter.3.cloned.1.call-done = bf16[1,2,32,4096]{3,2,1,0:T(8,128)(2,1)} async-done(((bf16[8,2,32,4096]{3,2,1,0:T(8,128)(2,1)}), bf16[1,2,32,4096]{3,2,1,0:T(8,128)(2,1)}) %reduce-scatter.3.cloned.1.call-update) | async-done | bytes 524304 | tf_op jit(solution)/shard_map/reduce_scatter | solution.py:208
  264.7 2.3 pad_maximum_fusion.3
  267.0 0.0 all-gather.6.cloned.1.call-update
  267.0 0.0 all-reduce.2.cloned.1.call-start
  267.1 8.4 %all-gather = f32[8,1,8,256]{3,2,1,0:T(8,128)S(1)} all-gather(f32[2,1,8,256]{3,2,1,0:T(8,128)S(1)} %copy-done.9), channel_id=2, replica_groups=mesh['section'=4,'dp'=8] {'section'}, dimensions={0}, use_global_device_ids=true | all-gather | bytes 81920 | tf_op jit(solution)/shard_map/all_gather | solution.py:139
  275.5 42.8 %all-gather.6.cloned.1.call-done = bf16[8,2,32,4096]{3,2,1,0:T(8,128)(2,1)} async-done(((bf16[2,2,32,4096]{3,2,1,0:T(8,128)(2,1)}), bf16[8,2,32,4096]{3,2,1,0:T(8,128)(2,1)}) %all-gather.6.cloned.1.call-update) | async-done | bytes 4194320 | tf_op jit(solution)/shard_map/all_gather | solution.py:210
  318.2 2.5 fusion.24
  320.7 2.2 copy.75
  322.9 1.3 copy.77
  324.2 0.0 copy-start.7
  324.2 2.2 copy.74
  326.4 1.3 copy.76
  327.7 0.0 copy-start.8
  327.8 1.5 fusion.27
  329.3 0.0 copy-start.10
  329.3 1.4 copy-done.8
  330.7 1.5 convolution_add_fusion
  332.2 0.1 fusion.17
  332.3 0.6 pad_maximum_fusion.4
  333.0 0.0 all-reduce.2.cloned.1.call-update
  333.0 4.7 %fusion.26 = f32[256,8192]{1,0:T(8,128)} fusion(bf16[128,256]{1,0:T(8,128)(2,1)S(1)} %bitcast.112, bf16[128,8192]{1,0:T(8,128)(2,1)S(1)} %bitcast.99), kind=kOutput, calls=%fused_computation.49 | convolution fusion | flops 536870912 | bytes 10551296 | tf_op jit(solution)/shard_map/dot_general | solution.py:217
  337.7 4.7 %fusion.25 = f32[256,8192]{1,0:T(8,128)} fusion(bf16[128,256]{1,0:T(8,128)(2,1)S(1)} %bitcast.113, bf16[128,8192]{1,0:T(8,128)(2,1)S(1)} %bitcast.101), kind=kOutput, calls=%fused_computation.48 | convolution fusion | flops 536870912 | bytes 10551296 | tf_op jit(solution)/shard_map/dot_general | solution.py:217
  342.4 40.9 %all-reduce.2.cloned.1.call-done = f32[66,256]{1,0:T(8,128)} async-done(((f32[66,256]{1,0:T(8,128)}), f32[66,256]{1,0:T(8,128)}) %all-reduce.2.cloned.1.call-update) | async-done | bytes 67600 | tf_op jit(solution)/shard_map/psum | solution.py:227
  383.3 1.3 slice.50
  384.5 1.3 dynamic-slice_bitcast_fusion
  385.9 0.8 copy.80
  (22 shorter events, 0.1 us)
Async XLA Ops:
  7.2 94.4 %all-gather.4.cloned.1.call-start = ((), (), s32[]{:S(2)}) async-start(), calls=%async_computation.2 | async-start | bytes 9437184 | tf_op jit(solution)/shard_map/all_gather | solution.py:153
  14.7 2.0 copy-start.13
  14.7 2.2 copy-start.11
  14.7 2.2 copy-start.12
  15.4 86.1 %copy-start.1 = (bf16[2,1,4,16,4096]{4,3,2,1,0:T(8,128)(2,1)S(1)}, bf16[2,1,4,16,4096]{4,3,2,1,0:T(8,128)(2,1)}, u32[]{:S(2)}) copy-start(bf16[2,1,4,16,4096]{4,3,2,1,0:T(8,128)(2,1)} %param.9) | copy-start | bytes 3145732
  15.4 86.1 %copy-start.2 = (bf16[4,16,4096]{2,1,0:T(8,128)(2,1)S(1)}, bf16[4,16,4096]{2,1,0:T(8,128)(2,1)}, u32[]{:S(2)}) copy-start(bf16[4,16,4096]{2,1,0:T(8,128)(2,1)} %grad.1) | copy-start | bytes 1572868
  16.6 196.8 %reduce-scatter.5.cloned.1.call-start = ((), (), s32[]{:S(2)}) async-start(), calls=%async_computation.4 | async-start | bytes 4718592 | tf_op jit(solution)/shard_map/reduce_scatter | solution.py:208
  101.5 3.4 copy-start
  162.8 1.5 copy-start.3
  166.7 1.2 copy-start.4
  166.7 98.0 %reduce-scatter.3.cloned.1.call-start = ((), (), s32[]{:S(2)}) async-start(), calls=%async_computation.3 | async-start | bytes 4718592 | tf_op jit(solution)/shard_map/reduce_scatter | solution.py:208
  171.7 95.3 %copy-start.9 = (f32[2,1,8,256]{3,2,1,0:T(8,128)S(1)}, f32[2,1,8,256]{3,2,1,0:T(8,128)}, u32[]{:S(2)}) copy-start(f32[2,1,8,256]{3,2,1,0:T(8,128)} %param.15) | copy-start | bytes 49156
  171.7 146.5 %all-gather.6.cloned.1.call-start = ((), (), s32[]{:S(2)}) async-start(), calls=%async_computation.5 | async-start | bytes 5242880 | tf_op jit(solution)/shard_map/all_gather | solution.py:210
  267.0 116.2 %all-reduce.2.cloned.1.call-start = ((), (), s32[]{:S(2)}) async-start(), calls=%async_computation.6 | async-start | bytes 147456 | tf_op jit(solution)/shard_map/psum | solution.py:227
  324.2 3.5 copy-start.7
  327.7 4.5 %copy-start.5 = (bf16[16,8,2,4096]{3,1,2,0:T(8,128)(2,1)}, bf16[16,8,2,4096]{3,1,2,0:T(8,128)(2,1)S(1)}, u32[]{:S(2)}) copy-start(bf16[16,8,2,4096]{3,1,2,0:T(8,128)(2,1)S(1)} %copy.76) | copy-start | bytes 6291460
  327.7 2.9 copy-start.8
  329.3 2.9 copy-start.10
  333.0 4.7 %copy-start.6 = (bf16[16,8,2,4096]{3,1,2,0:T(8,128)(2,1)S(1)}, bf16[16,8,2,4096]{3,1,2,0:T(8,128)(2,1)}, u32[]{:S(2)}) copy-start(bf16[16,8,2,4096]{3,1,2,0:T(8,128)(2,1)} %copy-done.5) | copy-start | bytes 6291460
Sparse Core Ops, SparseCore 0:
  16.7 84.7 all-gather.3
  166.8 46.5 reduce-scatter.4
  216.3 48.3 reduce-scatter.2
  267.1 51.0 all-gather.5
  333.1 50.0 all-reduce.1

commit v2 on v1

--- a/solution.py
+++ b/solution.py
@@ -224,7 +224,7 @@
             jnp.sum(d_pre, axis=(0, 1, 3)),
         ]
     )
-    sums = lax.psum(sums, "dp")
+    sums = jnp.sum(lax.all_gather(sums, "dp", axis=0), axis=0)
     d_task = sums[-tasks:]
     d_slot = lax.dynamic_slice_in_dim(
         sums, section_id * blocks * experts, blocks * experts

time: 395 us -> 365 us (0.924)
  waiting for transfers between devices: 261 us -> 220 us
  blocking collectives: 8.39 us -> 23.5 us
    psum x1 -> x0, waiting for transfers between devices: 40.9 us -> none  [on_device(): sums = lax.psum(sums, 'dp')]
    all_gather x0 -> x1, blocking collectives: none -> 15.1 us  [on_device(): sums = jnp.sum(lax.all_gather(sums, 'dp', axis=0), axis=0)]
    unnamed x31 -> x27, local copies, waits for them, and re-layouts: 9.37 us -> 8.6 us
  transfers between devices with their start and end apart: 5 -> 4, of which waited for: 5 -> 4; matrix products, arithmetic and copies ran while one was open for 4% -> 1% of each run, Pallas kernels for 0% -> 0%
where the time goes in v2:
time: 365 us
  waiting for transfers between devices  220 us (60%)
  Pallas kernels  57.9 us (16%)
  blocking collectives  23.5 us (6%)
  matrix products  21.4 us (6%)
  local copies, waits for them, and re-layouts  19.8 us (5%)
  between operations  14 us (4%)
  other arithmetic  8.17 us (2%)
    reduce_scatter x2, waiting for transfers between devices, on_device(): lax.psum_scatter(pair, 'dp', scatter_dimension=0, tiled=True)  92.9 us
    all_gather x1, waiting for transfers between devices, on_device(): adapt = lax.all_gather(shard, 'dp', axis=0, tiled=True)  83.9 us
    pallas_call x1, Pallas kernels, on_device(): pl.pallas_call(functools.partial(relay, sections, blocks, micro, min(widt...  57.9 us
    all_gather x1, waiting for transfers between devices, on_device(): every = lax.all_gather(own, 'section', axis=0, tiled=True)  42.8 us
    all_gather x1, blocking collectives, on_device(): sums = jnp.sum(lax.all_gather(sums, 'dp', axis=0), axis=0)  15.1 us
    dot_general x2, matrix products, on_device(): lax.dot_general(cond_all, every[which], tn, preferred_element_type=jnp.fl...  9.34 us
    unnamed x27, local copies, waits for them, and re-layouts  8.6 us
    all_gather x1, blocking collectives, on_device(): slots = lax.all_gather(slot_embed[:, 0], 'section', axis=0)  8.39 us
  transfers between devices with their start and end apart: 4, of which 4 were waited for; matrix products, arithmetic and copies ran while one was open for 1% of the time, Pallas kernels for 0%

profile of v2, /device:TPU:0, one launch (start us, length us, event | category | flops | bytes accessed | tf_op | source)
XLA Modules:
  0.0 364.6 jit_solution(6554014306756747214)
XLA Ops:
  7.2 0.0 all-gather.6.cloned.1.call-start
  7.2 0.7 broadcast_add_fusion
  8.0 3.0 convolution_convert_fusion
  11.0 0.4 reshape.122
  11.4 0.3 copy.68
  11.7 3.0 convolution_convert_fusion.1
  14.7 0.0 copy-start.11
  14.7 0.0 copy-start.9
  14.7 0.0 copy-start.10
  14.7 0.4 reshape.121
  15.1 0.3 copy.67
  15.4 0.0 copy-start.1
  15.4 0.0 copy-start.2
  15.4 0.1 pad_maximum_fusion.2
  15.5 1.0 copy.69
  16.6 0.0 all-gather.6.cloned.1.call-update
  16.6 0.0 reduce-scatter.5.cloned.1.call-start
  16.7 0.1 fusion.22
  16.7 0.1 mul.78
  16.8 0.1 mul.79
  16.9 0.1 broadcast_multiply_fusion
  17.0 0.1 copy.66
  17.1 0.1 tile.8
  17.2 0.4 tile.9.cols
  17.6 83.9 %all-gather.6.cloned.1.call-done.adapt = bf16[8,4,32,4096]{3,2,1,0:T(8,128)(2,1)} async-done(((bf16[1,4,32,4096]{3,2,1,0:T(8,128)(2,1)}), bf16[8,4,32,4096]{3,2,1,0:T(8,128)(2,1)}) %all-gather.6.cloned.1.call-update) | async-done | bytes 8388624 | tf_op jit(solution)/shard_map/all_gather | solution.py:153
  101.5 0.0 copy-done.1
  101.5 3.4 copy-done
  104.9 57.9 %relay.1 = (bf16[4,16,4096]{2,1,0:T(8,128)(2,1)S(1)}, bf16[8,16,4096]{2,1,0:T(8,128)(2,1)S(1)}, bf16[8,16,4096]{2,1,0:T(8,128)(2,1)S(1)}, bf16[8,16,256]{2,1,0:T(8,128)(2,1)S(1)}, bf16[8,16,256]{2,1,0:T(8,128)(2,1)S(1)}) custom-call(bf16[8,16,4096]{2,1,0:T(8,128)(2,1)S(1)} %bitcast.98, bf16[4,16,4096]{2,1,0:T(8,128)(2,1)S(1)} %copy-done.2, ...), custom_call_target="tpu_custom_call" | custom-call | tf_op jit(solution)/shard_map/relay/pallas_call | solution.py:168
  162.8 0.0 copy-start.3
  162.8 0.7 fusion.6
  163.5 0.7 fusion.7
  164.3 2.4 pad_maximum_fusion.1
  166.7 0.0 reduce-scatter.5.cloned.1.call-update
  166.7 0.0 reduce-scatter.3.cloned.1.call-start
  166.7 1.1 copy-done.4
  167.9 0.7 fusion.4
  168.6 0.7 fusion.5
  169.3 2.4 pad_maximum_fusion
  171.7 0.0 reduce-scatter.3.cloned.1.call-update
  171.7 0.0 all-gather.8.cloned.1.call-start
  171.8 41.6 %reduce-scatter.5.cloned.1.call-done = bf16[1,2,32,4096]{3,2,1,0:T(8,128)(2,1)} async-done(((bf16[8,2,32,4096]{3,2,1,0:T(8,128)(2,1)}), bf16[1,2,32,4096]{3,2,1,0:T(8,128)(2,1)}) %reduce-scatter.5.cloned.1.call-update) | async-done | bytes 524304 | tf_op jit(solution)/shard_map/reduce_scatter | solution.py:208
  213.4 51.3 %reduce-scatter.3.cloned.1.call-done = bf16[1,2,32,4096]{3,2,1,0:T(8,128)(2,1)} async-done(((bf16[8,2,32,4096]{3,2,1,0:T(8,128)(2,1)}), bf16[1,2,32,4096]{3,2,1,0:T(8,128)(2,1)}) %reduce-scatter.3.cloned.1.call-update) | async-done | bytes 524304 | tf_op jit(solution)/shard_map/reduce_scatter | solution.py:208
  264.7 2.3 pad_maximum_fusion.3
  267.0 0.0 all-gather.8.cloned.1.call-update
  267.0 8.4 %all-gather = f32[8,1,8,256]{3,2,1,0:T(8,128)S(1)} all-gather(f32[2,1,8,256]{3,2,1,0:T(8,128)S(1)} %copy-done.7), channel_id=2, replica_groups=mesh['section'=4,'dp'=8] {'section'}, dimensions={0}, use_global_device_ids=true | all-gather | bytes 81920 | tf_op jit(solution)/shard_map/all_gather | solution.py:139
  275.4 42.8 %all-gather.8.cloned.1.call-done = bf16[8,2,32,4096]{3,2,1,0:T(8,128)(2,1)} async-done(((bf16[2,2,32,4096]{3,2,1,0:T(8,128)(2,1)}), bf16[8,2,32,4096]{3,2,1,0:T(8,128)(2,1)}) %all-gather.8.cloned.1.call-update) | async-done | bytes 4194320 | tf_op jit(solution)/shard_map/all_gather | solution.py:210
  318.2 2.5 fusion.24
  320.7 2.2 copy.75
  322.9 1.3 copy.77
  324.2 0.0 copy-start.5
  324.2 2.2 copy.74
  326.4 1.3 copy.76
  327.7 0.0 copy-start.6
  327.7 1.5 fusion.27
  329.3 0.0 copy-start.8
  329.3 0.6 copy-done.6
  329.9 1.6 convolution_add_fusion
  331.5 0.1 fusion.17
  331.6 4.7 %fusion.26 = f32[256,8192]{1,0:T(8,128)} fusion(bf16[128,256]{1,0:T(8,128)(2,1)S(1)} %bitcast.114, bf16[128,8192]{1,0:T(8,128)(2,1)S(1)} %bitcast.101), kind=kOutput, calls=%fused_computation.49 | convolution fusion | flops 536870912 | bytes 10551296 | tf_op jit(solution)/shard_map/dot_general | solution.py:217
  336.3 4.7 %fusion.25 = f32[256,8192]{1,0:T(8,128)} fusion(bf16[128,256]{1,0:T(8,128)(2,1)S(1)} %bitcast.115, bf16[128,8192]{1,0:T(8,128)(2,1)S(1)} %bitcast.103), kind=kOutput, calls=%fused_computation.48 | convolution fusion | flops 536870912 | bytes 10551296 | tf_op jit(solution)/shard_map/dot_general | solution.py:217
  341.0 15.1 %all-gather.2 = f32[8,66,256]{2,1,0:T(8,128)S(1)} all-gather(f32[1,66,256]{2,1,0:T(8,128)S(1)} %maximum_bitcast_fusion), channel_id=3, replica_groups=mesh['section'=4,'dp'=8] {'dp'}, dimensions={0}, use_global_device_ids=true | all-gather | bytes 608256 | tf_op jit(solution)/shard_map/all_gather | solution.py:227
  356.1 0.6 slice.50
  356.7 0.6 dynamic-slice_bitcast_fusion
  357.3 0.8 copy.79
  (17 shorter events, 0.1 us)
Async XLA Ops:
  7.2 94.4 %all-gather.6.cloned.1.call-start = ((), (), s32[]{:S(2)}) async-start(), calls=%async_computation.2 | async-start | bytes 9437184 | tf_op jit(solution)/shard_map/all_gather | solution.py:153
  14.7 2.0 copy-start.11
  14.7 2.2 copy-start.9
  14.7 2.2 copy-start.10
  15.4 86.1 %copy-start.1 = (bf16[2,1,4,16,4096]{4,3,2,1,0:T(8,128)(2,1)S(1)}, bf16[2,1,4,16,4096]{4,3,2,1,0:T(8,128)(2,1)}, u32[]{:S(2)}) copy-start(bf16[2,1,4,16,4096]{4,3,2,1,0:T(8,128)(2,1)} %param.9) | copy-start | bytes 3145732
  15.4 86.1 %copy-start.2 = (bf16[4,16,4096]{2,1,0:T(8,128)(2,1)S(1)}, bf16[4,16,4096]{2,1,0:T(8,128)(2,1)}, u32[]{:S(2)}) copy-start(bf16[4,16,4096]{2,1,0:T(8,128)(2,1)} %grad.1) | copy-start | bytes 1572868
  16.6 196.8 %reduce-scatter.5.cloned.1.call-start = ((), (), s32[]{:S(2)}) async-start(), calls=%async_computation.4 | async-start | bytes 4718592 | tf_op jit(solution)/shard_map/reduce_scatter | solution.py:208
  101.5 3.4 copy-start
  162.8 1.5 copy-start.3
  166.7 1.2 copy-start.4
  166.7 98.0 %reduce-scatter.3.cloned.1.call-start = ((), (), s32[]{:S(2)}) async-start(), calls=%async_computation.3 | async-start | bytes 4718592 | tf_op jit(solution)/shard_map/reduce_scatter | solution.py:208
  171.7 95.3 %copy-start.7 = (f32[2,1,8,256]{3,2,1,0:T(8,128)S(1)}, f32[2,1,8,256]{3,2,1,0:T(8,128)}, u32[]{:S(2)}) copy-start(f32[2,1,8,256]{3,2,1,0:T(8,128)} %param.15) | copy-start | bytes 49156
  171.7 146.5 %all-gather.8.cloned.1.call-start = ((), (), s32[]{:S(2)}) async-start(), calls=%async_computation.5 | async-start | bytes 5242880 | tf_op jit(solution)/shard_map/all_gather | solution.py:210
  324.2 3.5 copy-start.5
  327.7 2.2 copy-start.6
  329.3 2.3 copy-start.8
Sparse Core Ops, SparseCore 0:
  16.7 84.7 all-gather.5
  166.8 46.5 reduce-scatter.4
  216.3 48.3 reduce-scatter.2
  267.1 51.0 all-gather.7
